TPU v7x, 32 devices: a whole 2x2x4 slice. The times are simulated.
32 devices in a mesh: sp: 4 (over y, x), fsdp: 8 (over z, core).
Axes of the slice: x: 2, y: 2, z: 4, core: 2. Of those that a mesh axis runs over, the one named last changes fastest.
Arguments:
- tokens: bfloat16 [2, 8, 1536, 1024], P(None, 'fsdp', 'sp'), may hold values from -6 to 6
- cotangent: bfloat16 [2, 8, 1536, 1024], P(None, 'fsdp', 'sp'), may hold values from -6 to 6
- destination: int32 [2, 8, 1536], P(None, 'fsdp', 'sp'), may hold values from 0 to 3071, as said below
- seq_lengths: int32 [2, 8, 3], P(None, 'fsdp'), may hold values from 1 to 1024, 1536 in all within a row
- qkv_weight: bfloat16 [1024, 3072], P('fsdp'), may hold values from -0.1875 to 0.1875
- output_weight: bfloat16 [1024, 1024], P('fsdp'), may hold values from -3 to 3
- input_weight: bfloat16 [1024, 5248], P('fsdp'), may hold values from -0.1875 to 0.1875
- mlp_weight: bfloat16 [2624, 1024], P(None, 'fsdp'), may hold values from -0.125 to 0.125
- first_gain: bfloat16 [1024], P('fsdp'), may hold values from 0.25 to 1.75
- second_gain: bfloat16 [1024], P('fsdp'), may hold values from 0.25 to 1.75
Outputs:
- layer_output: bfloat16 [2, 8, 1536, 1024], P(None, 'fsdp', 'sp')
- input_grad: bfloat16 [2, 8, 1536, 1024], P(None, 'fsdp', 'sp')
- qkv_weight_grad: float32 [1024, 3072], P('fsdp')
- output_weight_grad: float32 [1024, 1024], P('fsdp')
- input_weight_grad: float32 [1024, 5248], P('fsdp')
- mlp_weight_grad: float32 [2624, 1024], P(None, 'fsdp')
- first_gain_grad: float32 [1024], P('fsdp')
- second_gain_grad: float32 [1024], P('fsdp')
Inputs may be any that keep to these rules, and one draw needn't show every extreme that they name: destination[b, f, p] = g * 384 + r sends the row to place (p // 384) * 384 + r of group g; for each b and each block of 384 places with the same p // 384, over all f these places are each reached exactly once, and the rows of one f in that block send exactly 48 rows to each group. `seq_lengths`: the lengths of one group sum to 1536.
All inputs are finite; a program needn't handle non-finite values.
Results may differ from a plain program's by a relative error of at most 0.017.
Values may be sent and summed in bfloat16 or wider, within the bound.
A program may use at most 384 MiB of HBM per device.

v0:
```python
from functools import partial

import jax
import jax.numpy as jnp
from jax import lax
from jax.sharding import PartitionSpec as P

HEADS = 16
HEAD_DIM = 64
FF = 2624
N_MB = 2


norm_epsilon = 1e-05
rotary_base = 160000.0
masked_score = -1e30


def layer_norm(values, norm_gain):
    centre = values - jnp.mean(values, axis=-1, keepdims=True)
    spread = jnp.mean(centre * centre, axis=-1, keepdims=True)
    return centre * lax.rsqrt(spread + norm_epsilon) * norm_gain


def rotary_tables(places, head_width):
    exponents = jnp.arange(0, head_width, 2).astype(jnp.float32) / head_width
    inverse_freq = 1.0 / rotary_base**exponents
    angles = places.astype(jnp.float32)[:, None] * inverse_freq[None, :]
    angles = jnp.concatenate([angles, angles], axis=-1)
    return (jnp.cos(angles), jnp.sin(angles))


def rotary(values, cosine_table, sine_table):
    half_width = values.shape[-1] // 2
    table_shape = (values.shape[0],) + (1,) * (values.ndim - 2) + (values.shape[-1],)
    turned = jnp.concatenate([-values[..., half_width:], values[..., :half_width]], axis=-1)
    return values * cosine_table.reshape(table_shape) + turned * sine_table.reshape(table_shape)


def sequence_layout(lengths_row, positions):
    seq_ends = jnp.cumsum(lengths_row)
    passed = (positions[:, None] >= seq_ends[None, :]).astype(jnp.int32)
    seq_ids = jnp.sum(passed, axis=1)
    seq_starts = jnp.sum(passed * lengths_row[None, :], axis=1)
    return (seq_ids, positions - seq_starts)


def gated(gate_in, up_in):
    return jax.nn.gelu(gate_in, approximate=False) * up_in


def gather_weights(qkv_weight, output_weight, input_weight, mlp_weight, first_gain, second_gain):
    return (
        lax.all_gather(qkv_weight, "fsdp", axis=0, tiled=True),
        lax.all_gather(output_weight, "fsdp", axis=0, tiled=True),
        lax.all_gather(input_weight, "fsdp", axis=0, tiled=True),
        lax.all_gather(mlp_weight, "fsdp", axis=1, tiled=True),
        lax.all_gather(first_gain, "fsdp", axis=0, tiled=True),
        lax.all_gather(second_gain, "fsdp", axis=0, tiled=True),
    )


def reduce_grads(gradients):
    return (
        lax.psum_scatter(gradients[0], "fsdp", scatter_dimension=0, tiled=True),
        lax.psum_scatter(gradients[1], "fsdp", scatter_dimension=0, tiled=True),
        lax.psum_scatter(gradients[2], "fsdp", scatter_dimension=0, tiled=True),
        lax.psum_scatter(gradients[3], "fsdp", scatter_dimension=0, tiled=True),
        lax.psum_scatter(gradients[4], "fsdp", scatter_dimension=1, tiled=True),
        lax.psum_scatter(gradients[5], "fsdp", scatter_dimension=0, tiled=True),
        lax.psum_scatter(gradients[6], "fsdp", scatter_dimension=0, tiled=True),
    )


def micro_batch(block_tokens, block_cot, block_dest, lengths_row, gathered):
    qkv_full, out_full, in_full, mlp_full, gain_one_low, gain_two_low = gathered
    gain_one = gain_one_low.astype(jnp.float32)
    gain_two = gain_two_low.astype(jnp.float32)
    local_rows, model_width = block_tokens.shape
    sp_count = lax.axis_size("sp")
    local_heads = HEADS // sp_count
    group_rows = local_rows * sp_count
    sort_order = jnp.argsort(block_dest)
    outgoing = (block_tokens[sort_order], block_cot[sort_order], block_dest[sort_order])
    got_tokens, got_cot, got_dest = (
        lax.all_to_all(outgoing[0], "fsdp", split_axis=0, concat_axis=0, tiled=True),
        lax.all_to_all(outgoing[1], "fsdp", split_axis=0, concat_axis=0, tiled=True),
        lax.all_to_all(outgoing[2], "fsdp", split_axis=0, concat_axis=0, tiled=True),
    )
    slot_rows = got_dest % local_rows
    placing = jnp.argsort(slot_rows)
    owned = got_tokens[placing].astype(jnp.float32)
    cot_low = got_cot[placing]
    owned_cot = cot_low.astype(jnp.float32)
    local_positions = lax.axis_index("sp") * local_rows + jnp.arange(local_rows, dtype=jnp.int32)
    local_places = sequence_layout(lengths_row, local_positions)[1]
    seq_ids = sequence_layout(lengths_row, jnp.arange(group_rows, dtype=jnp.int32))[0]
    cosine_table, sine_table = rotary_tables(local_places, HEAD_DIM)
    normed_one, norm_one_pullback = jax.vjp(layer_norm, owned, gain_one)
    first_low = normed_one.astype(jnp.bfloat16)
    projected = jnp.dot(first_low, qkv_full, preferred_element_type=jnp.float32).reshape(
        local_rows, 3, HEADS, HEAD_DIM
    )
    rotated_pair, rotary_pullback = jax.vjp(
        partial(rotary, cosine_table=cosine_table, sine_table=sine_table), projected[:, :2]
    )
    stacked = jnp.concatenate([rotated_pair, projected[:, 2:]], axis=1).astype(jnp.bfloat16)
    stacked = stacked.reshape(local_rows, 3, sp_count, local_heads * HEAD_DIM)
    by_heads = lax.all_to_all(stacked, "sp", split_axis=2, concat_axis=0, tiled=True)
    query_heads = by_heads[:, 0, 0].reshape(group_rows, local_heads, HEAD_DIM)
    key_heads = by_heads[:, 1, 0].reshape(group_rows, local_heads, HEAD_DIM)
    value_heads = by_heads[:, 2, 0].reshape(group_rows, local_heads, HEAD_DIM)
    row_block = min(512, group_rows)
    score_scale = HEAD_DIM ** (-0.5)
    mixed_blocks = []
    log_totals = []
    for block_start in range(0, group_rows, row_block):
        block_queries = query_heads[block_start : block_start + row_block]
        same_seq = seq_ids[block_start : block_start + row_block][:, None] == seq_ids[None, :]
        raw_scores = (
            jnp.einsum("qhd,khd->hqk", block_queries, key_heads, preferred_element_type=jnp.float32)
            * score_scale
        )
        masked = jnp.where(same_seq[None], raw_scores, masked_score)
        row_max = jnp.max(masked, axis=-1, keepdims=True)
        exponent_terms = jnp.exp(masked - row_max)
        row_total = jnp.sum(exponent_terms, axis=-1, keepdims=True)
        softmax_low = (exponent_terms / row_total).astype(jnp.bfloat16)
        mixed_blocks.append(
            jnp.einsum("hqk,khd->qhd", softmax_low, value_heads, preferred_element_type=jnp.float32)
        )
        log_totals.append(row_max + jnp.log(row_total))
    attended_heads = jnp.concatenate(mixed_blocks, axis=0).astype(jnp.bfloat16)
    log_total = jnp.concatenate(log_totals, axis=1)
    attended = lax.all_to_all(
        attended_heads.reshape(group_rows, 1, local_heads * HEAD_DIM),
        "sp",
        split_axis=0,
        concat_axis=1,
        tiled=True,
    ).reshape(local_rows, model_width)
    middle = owned + jnp.dot(attended, out_full, preferred_element_type=jnp.float32)
    normed_two, norm_two_pullback = jax.vjp(layer_norm, middle, gain_two)
    second_low = normed_two.astype(jnp.bfloat16)
    lifted = jnp.dot(second_low, in_full, preferred_element_type=jnp.float32)
    gated_value, gate_pullback = jax.vjp(gated, lifted[:, :FF], lifted[:, FF:])
    hidden = gated_value.astype(jnp.bfloat16)
    result_low = (middle + jnp.dot(hidden, mlp_full, preferred_element_type=jnp.float32)).astype(
        jnp.bfloat16
    )
    mlp_grad = jnp.einsum("rf,rd->fd", hidden, cot_low, preferred_element_type=jnp.float32)
    grad_hidden = jnp.einsum("rd,fd->rf", cot_low, mlp_full, preferred_element_type=jnp.float32)
    grad_gate, grad_up = gate_pullback(grad_hidden)
    grad_lifted = jnp.concatenate([grad_gate, grad_up], axis=1).astype(jnp.bfloat16)
    gate_grad = jnp.einsum(
        "rd,rf->df", second_low, grad_lifted[:, :FF], preferred_element_type=jnp.float32
    )
    up_grad = jnp.einsum(
        "rd,rf->df", second_low, grad_lifted[:, FF:], preferred_element_type=jnp.float32
    )
    grad_two = jnp.einsum("rf,df->rd", grad_lifted, in_full, preferred_element_type=jnp.float32)
    grad_middle_norm, second_gain_grad = norm_two_pullback(grad_two)
    grad_middle = owned_cot + grad_middle_norm
    grad_branch = grad_middle.astype(jnp.bfloat16)
    output_grad = jnp.einsum("rd,re->de", attended, grad_branch, preferred_element_type=jnp.float32)
    grad_attended = jnp.einsum(
        "re,de->rd", grad_branch, out_full, preferred_element_type=jnp.float32
    ).astype(jnp.bfloat16)
    grad_heads_in = lax.all_to_all(
        grad_attended.reshape(local_rows, sp_count, local_heads * HEAD_DIM),
        "sp",
        split_axis=1,
        concat_axis=0,
        tiled=True,
    )
    grad_heads_in = grad_heads_in.reshape(group_rows, local_heads, HEAD_DIM)
    grad_query_blocks = []
    grad_keys = jnp.zeros((group_rows, local_heads, HEAD_DIM), jnp.float32)
    grad_values = jnp.zeros((group_rows, local_heads, HEAD_DIM), jnp.float32)
    for block_start in range(0, group_rows, row_block):
        block_queries = query_heads[block_start : block_start + row_block]
        block_grad_out = grad_heads_in[block_start : block_start + row_block]
        same_seq = seq_ids[block_start : block_start + row_block][:, None] == seq_ids[None, :]
        raw_scores = (
            jnp.einsum("qhd,khd->hqk", block_queries, key_heads, preferred_element_type=jnp.float32)
            * score_scale
        )
        masked = jnp.where(same_seq[None], raw_scores, masked_score)
        softmax_full = jnp.exp(masked - log_total[:, block_start : block_start + row_block])
        softmax_low = softmax_full.astype(jnp.bfloat16)
        grad_values = grad_values + jnp.einsum(
            "hqk,qhd->khd", softmax_low, block_grad_out, preferred_element_type=jnp.float32
        )
        grad_probs = jnp.einsum(
            "qhd,khd->hqk", block_grad_out, value_heads, preferred_element_type=jnp.float32
        )
        weighted_sum = jnp.sum(softmax_full * grad_probs, axis=-1, keepdims=True)
        grad_scores = (softmax_full * (grad_probs - weighted_sum)).astype(jnp.bfloat16)
        grad_query_blocks.append(
            jnp.einsum("hqk,khd->qhd", grad_scores, key_heads, preferred_element_type=jnp.float32)
            * score_scale
        )
        grad_keys = (
            grad_keys
            + jnp.einsum(
                "hqk,qhd->khd", grad_scores, block_queries, preferred_element_type=jnp.float32
            )
            * score_scale
        )
    grad_queries = jnp.concatenate(grad_query_blocks, axis=0)
    grad_stack = jnp.stack([grad_queries, grad_keys, grad_values], axis=1).astype(jnp.bfloat16)
    grad_stack = grad_stack.reshape(group_rows, 3, 1, local_heads * HEAD_DIM)
    grad_tokens_qkv = lax.all_to_all(
        grad_stack, "sp", split_axis=0, concat_axis=2, tiled=True
    ).reshape(local_rows, 3, HEADS, HEAD_DIM)
    (grad_pair,) = rotary_pullback(grad_tokens_qkv[:, :2].astype(jnp.float32))
    grad_projected = jnp.concatenate(
        [grad_pair, grad_tokens_qkv[:, 2:].astype(jnp.float32)], axis=1
    )
    grad_projected = grad_projected.reshape(local_rows, 3 * model_width).astype(jnp.bfloat16)
    qkv_grad = jnp.einsum(
        "rd,re->de", first_low, grad_projected, preferred_element_type=jnp.float32
    )
    grad_one = jnp.einsum("re,de->rd", grad_projected, qkv_full, preferred_element_type=jnp.float32)
    grad_owned_norm, first_gain_grad = norm_one_pullback(grad_one)
    grad_owned = (grad_middle + grad_owned_norm).astype(jnp.bfloat16)
    returned = (result_low[slot_rows], grad_owned[slot_rows])
    back_result, back_grad = (
        lax.all_to_all(returned[0], "fsdp", split_axis=0, concat_axis=0, tiled=True),
        lax.all_to_all(returned[1], "fsdp", split_axis=0, concat_axis=0, tiled=True),
    )
    restore = jnp.argsort(sort_order)
    gradients = (
        qkv_grad,
        output_grad,
        gate_grad,
        up_grad,
        mlp_grad,
        first_gain_grad,
        second_gain_grad,
    )
    return (back_result[restore], back_grad[restore], gradients)


def on_device(
    tokens,
    cotangent,
    destination,
    seq_lengths,
    qkv_weight,
    output_weight,
    input_weight,
    mlp_weight,
    first_gain,
    second_gain,
):
    result_list = []
    grad_list = []
    for batch_index in range(N_MB):
        gathered = gather_weights(
            qkv_weight, output_weight, input_weight, mlp_weight, first_gain, second_gain
        )
        result_rows, grad_rows, gradients = micro_batch(
            tokens[batch_index, 0],
            cotangent[batch_index, 0],
            destination[batch_index, 0],
            seq_lengths[batch_index, 0],
            gathered,
        )
        result_list.append(result_rows)
        grad_list.append(grad_rows)
        shares = reduce_grads(gradients)
        summed = shares if batch_index == 0 else jax.tree.map(jnp.add, summed, shares)
    summed = (
        lax.psum(summed[0].astype(jnp.bfloat16), "sp").astype(jnp.float32),
        lax.psum(summed[1].astype(jnp.bfloat16), "sp").astype(jnp.float32),
        lax.psum(summed[2].astype(jnp.bfloat16), "sp").astype(jnp.float32),
        lax.psum(summed[3].astype(jnp.bfloat16), "sp").astype(jnp.float32),
        lax.psum(summed[4].astype(jnp.bfloat16), "sp").astype(jnp.float32),
        lax.psum(summed[5].astype(jnp.bfloat16), "sp").astype(jnp.float32),
        lax.psum(summed[6].astype(jnp.bfloat16), "sp").astype(jnp.float32),
    )
    layer_output = jnp.stack(result_list, axis=0)[:, None]
    input_grad = jnp.stack(grad_list, axis=0)[:, None]
    input_weight_grad = jnp.concatenate([summed[2], summed[3]], axis=1)
    return (
        layer_output,
        input_grad,
        summed[0],
        summed[1],
        input_weight_grad,
        summed[4],
        summed[5],
        summed[6],
    )


def solution(mesh):
    placed = (
        P(None, "fsdp", "sp", None),
        P(None, "fsdp", "sp", None),
        P(None, "fsdp", "sp"),
        P(None, "fsdp", None),
        P("fsdp", None),
        P("fsdp", None),
        P("fsdp", None),
        P(None, "fsdp"),
        P("fsdp"),
        P("fsdp"),
    )
    return jax.shard_map(
        on_device,
        mesh=mesh,
        in_specs=placed,
        out_specs=(
            P(None, "fsdp", "sp", None),
            P(None, "fsdp", "sp", None),
            P("fsdp", None),
            P("fsdp", None),
            P("fsdp", None),
            P(None, "fsdp"),
            P("fsdp"),
            P("fsdp"),
        ),
        check_vma=False,
    )
```

profile of v0, /device:TPU:0, one launch (start us, length us, event | category | flops | bytes accessed | tf_op | source)
XLA Modules:
  0.0 1170.3 jit_solution(3862777523056577613)
XLA Ops:
  40.4 12.5 %all-gather = bf16[8,1,128]{2,1,0:T(2,128)(2,1)S(1)} all-gather(bf16[1,1,128]{2,1,0:T(2,128)(2,1)S(1)} %bitcast.388), channel_id=1, replica_groups=mesh['sp'=4,'fsdp'=8] {'fsdp'}, dimensions={0}, use_global_device_ids=true | all-gather | bytes 2304 | tf_op jit(solution)/shard_map/all_gather | solution.py:58
  70.1 22.4 %all-to-all-done.5 = bf16[8,48,1024]{2,1,0:T(8,128)(2,1)S(1)} async-done(((bf16[8,48,1024]{2,1,0:T(8,128)(2,1)}), bf16[8,48,1024]{2,1,0:T(8,128)(2,1)S(1)}, u32[]{:S(2)}, u32[]{:S(2)}) %all-to-all-start.5) | async-done | bytes 786464 | tf_op jit(solution)/shard_map/all_to_all | solution.py:86
  99.3 33.7 %all-to-all-done = bf16[8,48,1024]{2,1,0:T(8,128)(2,1)S(1)} async-done(((bf16[8,48,1024]{2,1,0:T(8,128)(2,1)}), bf16[8,48,1024]{2,1,0:T(8,128)(2,1)S(1)}, u32[]{:S(2)}, u32[]{:S(2)}) %all-to-all-start) | async-done | bytes 786464 | tf_op jit(solution)/shard_map/all_to_all | solution.py:86
  157.5 17.6 %all-to-all-done.7 = bf16[384,3,4,256]{0,3,1,2:T(8,128)(2,1)S(1)} async-done(((bf16[384,3,4,256]{0,3,1,2:T(8,128)(2,1)}), bf16[384,3,4,256]{0,3,1,2:T(8,128)(2,1)S(1)}, u32[]{:S(2)}, u32[]{:S(2)}) %all-to-all-start.7) | async-done | bytes 2359328 | tf_op jit(solution)/shard_map/all_to_all | solution.py:109
  197.4 10.9 all-to-all-done.2
  260.8 7.8 pad_maximum_fusion.7
  269.2 8.1 reduce.20
  332.9 15.0 %all-to-all-done.14 = bf16[8,48,1024]{2,1,0:T(8,128)(2,1)S(1)} async-done(((bf16[8,48,1024]{2,1,0:T(8,128)(2,1)}), bf16[8,48,1024]{2,1,0:T(8,128)(2,1)S(1)}, u32[]{:S(2)}, u32[]{:S(2)}) %all-to-all-start.14) | async-done | bytes 786464 | tf_op jit(solution)/shard_map/all_to_all | solution.py:87
  361.3 7.8 pad_maximum_fusion.6
  369.1 9.0 reduce.21
  384.2 9.7 all-gather.1
  414.7 10.9 fusion.193
  425.6 16.1 %add_convert_fusion.1 = (bf16[384,2624]{1,0:T(8,128)(2,1)S(1)}, f32[384,2624]{1,0:T(8,128)}, f32[384,2624]{1,0:T(8,128)}) fusion(f32[384,5248]{1,0:T(8,128)} %fusion.193, bf16[384,1024]{1,0:T(8,128)(2,1)S(1)} %copy-done.33, bf16[2624,1024]{1,0:T(8,128)(2,1)} %all-gather.13.cloned.1.call-done), kind=kOutput, calls=%fused_computation.95 | convolution fusion | flops 2137153536 | bytes 24297472 | tf_op jit(solution)/shard_map/rd,fd->rf/dot_general | solution.py:152
  441.7 9.3 multiply_convert_fusion.7
  451.0 11.2 multiply_reduce_fusion.7
  464.6 8.4 fusion.194
  473.0 13.8 %add_convert_fusion = (bf16[384,2624]{1,0:T(8,128)(2,1)}, f32[384,2624]{1,0:T(8,128)}, f32[384,2624]{1,0:T(8,128)}) fusion(f32[384,5248]{1,0:T(8,128)S(1)} %fusion.194, bf16[384,1024]{1,0:T(8,128)(2,1)S(1)} %copy-done.34, bf16[2624,1024]{1,0:T(8,128)(2,1)S(1)} %bitcast.391), kind=kOutput, calls=%fused_computation.93 | convolution fusion | flops 2137153536 | bytes 24297472 | tf_op jit(solution)/shard_map/rd,fd->rf/dot_general | solution.py:152
  486.9 8.4 multiply_convert_fusion.6
  496.7 11.0 multiply_reduce_fusion.6
  564.9 8.0 fusion.20
  572.8 9.1 multiply_reduce_fusion.4
  604.4 9.9 multiply_convert_fusion.5
  619.0 7.5 multiply_convert_fusion.4
  626.7 8.6 multiply_convert_fusion.3
  785.3 29.5 %all-to-all-done.16 = bf16[1536,3,1,256]{3,1,2,0:T(4,128)(2,1)} async-done(((bf16[1536,3,1,256]{3,1,2,0:T(4,128)(2,1)}), bf16[1536,3,1,256]{3,1,2,0:T(4,128)(2,1)}, u32[]{:S(2)}, u32[]{:S(2)}) %all-to-all-start.16) | async-done | bytes 2359328 | tf_op jit(solution)/shard_map/all_to_all | solution.py:213
  868.8 7.6 fusion.105
  876.4 10.3 all-to-all-done.9
  900.8 27.0 %reduce-scatter.14.cloned.1.call-done = f32[2624,128]{1,0:T(8,128)} async-done(((f32[2624,1024]{1,0:T(8,128)}), f32[2624,128]{1,0:T(8,128)}) %reduce-scatter.14.cloned.1.call-update) | async-done | bytes 1343504 | tf_op jit(solution)/shard_map/reduce_scatter | solution.py:69
  930.1 135.2 %reduce-scatter.6.cloned.1.call-done = f32[128,3072]{1,0:T(8,128)} async-done(((f32[1024,3072]{1,0:T(8,128)}), f32[128,3072]{1,0:T(8,128)}) %reduce-scatter.6.cloned.1.call-update) | async-done | bytes 1572880 | tf_op jit(solution)/shard_map/reduce_scatter | solution.py:65
  1079.8 18.1 %all-to-all-done.17 = bf16[8,48,1024]{2,1,0:T(8,128)(2,1)S(1)} async-done(((bf16[8,48,1024]{2,1,0:T(8,128)(2,1)}), bf16[8,48,1024]{2,1,0:T(8,128)(2,1)S(1)}, u32[]{:S(2)}, u32[]{:S(2)}) %all-to-all-start.17) | async-done | bytes 786464 | tf_op jit(solution)/shard_map/all_to_all | solution.py:230
  1118.5 17.3 %all-reduce.6 = (bf16[1024]{0:T(1024)(128)(2,1)S(1)}, bf16[1024]{0:T(1024)(128)(2,1)S(1)}) all-reduce(f32[1024]{0:T(1024)S(1)} %add.385, f32[1024]{0:T(1024)S(1)} %add.386), channel_id=14, replica_groups=mesh['sp'=4,'fsdp'=8] {'fsdp'}, use_global_device_ids=true, to_apply=%region_62.63.clone | all-reduce | flops 2048 | bytes 12288
  1135.9 10.3 all-reduce.7
  (685 shorter events, 610.1 us)
Async XLA Ops:
  7.2 128.5 %all-gather.7.cloned.1.call-start = ((), (), s32[]{:S(2)}) async-start(), calls=%async_computation.23 | async-start | bytes 7077888 | tf_op jit(solution)/shard_map/all_gather | solution.py:54
  7.9 399.5 %all-gather.9.cloned.1.call-start = ((), (), s32[]{:S(2)}) async-start(), calls=%async_computation.24 | async-start | bytes 2359296 | tf_op jit(solution)/shard_map/all_gather | solution.py:55
  8.7 406.1 %all-gather.11.cloned.1.call-start = ((), (), s32[]{:S(2)}) async-start(), calls=%async_computation.25 | async-start | bytes 12091392 | tf_op jit(solution)/shard_map/all_gather | solution.py:56
  17.4 15.1 %all-to-all-start.6 = ((s32[8,48,1]{1,2,0:T(1,128)}), s32[8,48,1]{1,2,0:T(1,128)S(1)}, u32[]{:S(2)}, u32[]{:S(2)}) async-start(s32[8,48,1]{1,2,0:T(1,128)} %bitcast.38), calls=%async_computation.6 | async-start | bytes 8192 | tf_op jit(solution)/shard_map/all_to_all | solution.py:88
  23.7 401.9 %all-gather.13.cloned.1.call-start = ((), (), s32[]{:S(2)}) async-start(), calls=%async_computation.26 | async-start | bytes 6045696 | tf_op jit(solution)/shard_map/all_gather | solution.py:57
  32.5 23.2 %all-to-all-start.1 = ((s32[8,48,1]{1,2,0:T(1,128)}), s32[8,48,1]{1,2,0:T(1,128)S(1)}, u32[]{:S(2)}, u32[]{:S(2)}) async-start(s32[8,48,1]{1,2,0:T(1,128)} %bitcast.3), calls=%async_computation.1 | async-start | bytes 8192 | tf_op jit(solution)/shard_map/all_to_all | solution.py:88
  37.7 104.3 %copy-start.88 = (f32[384,64]{0,1:T(8,128)}, f32[384,64]{0,1:T(8,128)S(1)}, u32[]{:S(2)}) copy-start(f32[384,64]{0,1:T(8,128)S(1)} %get-tuple-element.118) | copy-start | bytes 294916
  37.7 104.3 %copy-start.90 = (f32[384,64]{0,1:T(8,128)}, f32[384,64]{0,1:T(8,128)S(1)}, u32[]{:S(2)}) copy-start(f32[384,64]{0,1:T(8,128)S(1)} %get-tuple-element.119) | copy-start | bytes 294916
  55.7 36.8 %all-to-all-start.5 = ((bf16[8,48,1024]{2,1,0:T(8,128)(2,1)}), bf16[8,48,1024]{2,1,0:T(8,128)(2,1)S(1)}, u32[]{:S(2)}, u32[]{:S(2)}) async-start(bf16[8,48,1024]{2,1,0:T(8,128)(2,1)} %bitcast.36), calls=%async_computation.5 | async-start | bytes 1572864 | tf_op jit(solution)/shard_map/all_to_all | solution.py:86
  92.5 40.5 %all-to-all-start = ((bf16[8,48,1024]{2,1,0:T(8,128)(2,1)}), bf16[8,48,1024]{2,1,0:T(8,128)(2,1)S(1)}, u32[]{:S(2)}, u32[]{:S(2)}) async-start(bf16[8,48,1024]{2,1,0:T(8,128)(2,1)} %bitcast.1), calls=%async_computation | async-start | bytes 1572864 | tf_op jit(solution)/shard_map/all_to_all | solution.py:86
  144.7 30.4 %all-to-all-start.7 = ((bf16[384,3,4,256]{0,3,1,2:T(8,128)(2,1)}), bf16[384,3,4,256]{0,3,1,2:T(8,128)(2,1)S(1)}, u32[]{:S(2)}, u32[]{:S(2)}) async-start(bf16[384,3,4,256]{0,3,1,2:T(8,128)(2,1)} %copy.145), calls=%async_computation.7 | async-start | bytes 4718592 | tf_op jit(solution)/shard_map/all_to_all | solution.py:109
  176.5 31.9 %all-to-all-start.2 = ((bf16[384,3,4,256]{0,3,1,2:T(8,128)(2,1)}), bf16[384,3,4,256]{0,3,1,2:T(8,128)(2,1)}, u32[]{:S(2)}, u32[]{:S(2)}) async-start(bf16[384,3,4,256]{0,3,1,2:T(8,128)(2,1)} %copy.132), calls=%async_computation.2 | async-start | bytes 4718592 | tf_op jit(solution)/shard_map/all_to_all | solution.py:109
  208.3 113.5 %all-to-all-start.10 = ((bf16[8,48,1024]{2,1,0:T(8,128)(2,1)}), bf16[8,48,1024]{2,1,0:T(8,128)(2,1)S(1)}, u32[]{:S(2)}, u32[]{:S(2)}) async-start(bf16[8,48,1024]{2,1,0:T(8,128)(2,1)} %bitcast.69), calls=%async_computation.10 | async-start | bytes 1572864 | tf_op jit(solution)/shard_map/all_to_all | solution.py:87
  321.9 26.0 %all-to-all-start.14 = ((bf16[8,48,1024]{2,1,0:T(8,128)(2,1)}), bf16[8,48,1024]{2,1,0:T(8,128)(2,1)S(1)}, u32[]{:S(2)}, u32[]{:S(2)}) async-start(bf16[8,48,1024]{2,1,0:T(8,128)(2,1)} %bitcast.89), calls=%async_computation.14 | async-start | bytes 1572864 | tf_op jit(solution)/shard_map/all_to_all | solution.py:87
  347.9 32.2 %all-to-all-start.8 = ((bf16[4,2,49152]{2,1,0:T(2,128)(2,1)}), bf16[4,2,49152]{2,1,0:T(2,128)(2,1)}, u32[]{:S(2)}, u32[]{:S(2)}) async-start(bf16[4,2,49152]{2,1,0:T(2,128)(2,1)} %reshape.1070), calls=%async_computation.8 | async-start | bytes 1572864 | tf_op jit(solution)/shard_map/all_to_all | solution.py:135
  380.1 25.2 %all-to-all-start.3 = ((bf16[4,2,49152]{2,1,0:T(2,128)(2,1)}), bf16[4,2,49152]{2,1,0:T(2,128)(2,1)S(1)}, u32[]{:S(2)}, u32[]{:S(2)}) async-start(bf16[4,2,49152]{2,1,0:T(2,128)(2,1)} %reshape.1072), calls=%async_computation.3 | async-start | bytes 1572864 | tf_op jit(solution)/shard_map/all_to_all | solution.py:135
  384.2 510.3 %reduce-scatter.8.cloned.1.call-start = ((), (), s32[]{:S(2)}) async-start(), calls=%async_computation.28 | async-start | bytes 4718592 | tf_op jit(solution)/shard_map/reduce_scatter | solution.py:66
  410.5 116.3 %copy-start.14 = (f32[384,1024]{1,0:T(8,128)}, f32[384,1024]{1,0:T(8,128)S(1)}, u32[]{:S(2)}) copy-start(f32[384,1024]{1,0:T(8,128)S(1)} %get-tuple-element.157) | copy-start | bytes 4718596
  515.9 380.4 %reduce-scatter.12.cloned.1.call-start = ((), (), s32[]{:S(2)}) async-start(), calls=%async_computation.30 | async-start | bytes 12091392 | tf_op jit(solution)/shard_map/reduce_scatter | solution.py:68
  526.7 371.9 %reduce-scatter.10.cloned.1.call-start = ((), (), s32[]{:S(2)}) async-start(), calls=%async_computation.29 | async-start | bytes 12091392 | tf_op jit(solution)/shard_map/reduce_scatter | solution.py:67
  542.4 16.8 %all-to-all-start.11 = ((bf16[384,4,256]{2,0,1:T(8,128)(2,1)}), bf16[384,4,256]{2,0,1:T(8,128)(2,1)S(1)}, u32[]{:S(2)}, u32[]{:S(2)}) async-start(bf16[384,4,256]{2,0,1:T(8,128)(2,1)} %bitcast.333), calls=%async_computation.11 | async-start | bytes 1572864 | tf_op jit(solution)/shard_map/all_to_all | solution.py:169
  546.6 381.3 %reduce-scatter.14.cloned.1.call-start = ((), (), s32[]{:S(2)}) async-start(), calls=%async_computation.31 | async-start | bytes 12091392 | tf_op jit(solution)/shard_map/reduce_scatter | solution.py:69
  559.2 108.2 %all-to-all-start.15 = ((bf16[384,4,256]{2,0,1:T(8,128)(2,1)}), bf16[384,4,256]{2,0,1:T(8,128)(2,1)}, u32[]{:S(2)}, u32[]{:S(2)}) async-start(bf16[384,4,256]{2,0,1:T(8,128)(2,1)} %bitcast.250), calls=%async_computation.15 | async-start | bytes 1572864 | tf_op jit(solution)/shard_map/all_to_all | solution.py:169
  667.3 106.3 %all-to-all-start.12 = ((bf16[1536,3,1,256]{3,1,2,0:T(4,128)(2,1)}), bf16[1536,3,1,256]{3,1,2,0:T(4,128)(2,1)}, u32[]{:S(2)}, u32[]{:S(2)}) async-start(bf16[1536,3,1,256]{3,1,2,0:T(4,128)(2,1)} %pad_maximum_fusion), calls=%async_computation.12 | async-start | bytes 6291456 | tf_op jit(solution)/shard_map/all_to_all | solution.py:213
  773.6 41.2 %all-to-all-start.16 = ((bf16[1536,3,1,256]{3,1,2,0:T(4,128)(2,1)}), bf16[1536,3,1,256]{3,1,2,0:T(4,128)(2,1)}, u32[]{:S(2)}, u32[]{:S(2)}) async-start(bf16[1536,3,1,256]{3,1,2,0:T(4,128)(2,1)} %pad_maximum_fusion.1), calls=%async_computation.16 | async-start | bytes 6291456 | tf_op jit(solution)/shard_map/all_to_all | solution.py:213
  778.3 287.0 %reduce-scatter.6.cloned.1.call-start = ((), (), s32[]{:S(2)}) async-start(), calls=%async_computation.27 | async-start | bytes 14155776 | tf_op jit(solution)/shard_map/reduce_scatter | solution.py:65
  849.1 37.6 %all-to-all-start.9 = ((bf16[8,48,1024]{2,1,0:T(8,128)(2,1)}), bf16[8,48,1024]{2,1,0:T(8,128)(2,1)S(1)}, u32[]{:S(2)}, u32[]{:S(2)}) async-start(bf16[8,48,1024]{2,1,0:T(8,128)(2,1)} %bitcast.63), calls=%async_computation.9 | async-start | bytes 1572864 | tf_op jit(solution)/shard_map/all_to_all | solution.py:229
  886.7 186.8 %all-to-all-start.4 = ((bf16[8,48,1024]{2,1,0:T(8,128)(2,1)}), bf16[8,48,1024]{2,1,0:T(8,128)(2,1)S(1)}, u32[]{:S(2)}, u32[]{:S(2)}) async-start(bf16[8,48,1024]{2,1,0:T(8,128)(2,1)} %bitcast.340), calls=%async_computation.4 | async-start | bytes 1572864 | tf_op jit(solution)/shard_map/all_to_all | solution.py:229
  890.3 263.8 %all-reduce.11.cloned.1.call-start = ((), (), s32[]{:S(2)}) async-start(), calls=%async_computation.32 | async-start | bytes 6127616 | tf_op jit(solution)/shard_map/psum | solution.py:275
  900.8 166.9 %copy-start.136 = (f32[384]{0:T(512)S(1)}, f32[384]{0:T(512)}, u32[]{:S(2)}) copy-start(f32[384]{0:T(512)} %copy-done.135) | copy-start | bytes 4612
  1073.5 24.4 %all-to-all-start.17 = ((bf16[8,48,1024]{2,1,0:T(8,128)(2,1)}), bf16[8,48,1024]{2,1,0:T(8,128)(2,1)S(1)}, u32[]{:S(2)}, u32[]{:S(2)}) async-start(bf16[8,48,1024]{2,1,0:T(8,128)(2,1)} %bitcast.342), calls=%async_computation.17 | async-start | bytes 1572864 | tf_op jit(solution)/shard_map/all_to_all | solution.py:230
  1097.9 51.4 %all-to-all-start.13 = ((bf16[8,48,1024]{2,1,0:T(8,128)(2,1)}), bf16[8,48,1024]{2,1,0:T(8,128)(2,1)S(1)}, u32[]{:S(2)}, u32[]{:S(2)}) async-start(bf16[8,48,1024]{2,1,0:T(8,128)(2,1)} %bitcast.341), calls=%async_computation.13 | async-start | bytes 1572864 | tf_op jit(solution)/shard_map/all_to_all | solution.py:230
  (175 other events, 2050.6 us)
Sparse Core Ops, SparseCore 0:
  9.6 82.3 all-gather.6
  93.7 42.0 all-gather.8
  137.4 117.1 all-gather.10
  256.0 55.8 all-gather.12
  516.1 48.7 reduce-scatter.7
  567.1 110.2 reduce-scatter.11
  679.7 110.2 reduce-scatter.9
  792.3 135.5 reduce-scatter.13
  930.1 135.1 reduce-scatter.5
  1069.5 84.5 all-reduce.10
where the time goes:
time: 1180 us; the launch traced here: 1170 us
  waiting for transfers between devices  324 us (27%)
  matrix products  318 us (27%)
  other arithmetic  207 us (18%)
  local copies, waits for them, and re-layouts  175 us (15%)
  starting transfers between devices  79.4 us (7%)
  blocking collectives  49.8 us (4%)
  between operations  17.9 us (2%)
    reduce_scatter x1, waiting for transfers between devices, reduce_grads(): lax.psum_scatter(gradients[0], 'fsdp', scatter_dimension=0, tiled=True)  135 us
    all_to_all x2, waiting for transfers between devices, micro_batch(): lax.all_to_all(outgoing[0], 'fsdp', split_axis=0, concat_axis=0, tiled=True)  56.2 us
    convert_element_type x6, other arithmetic, micro_batch(): (softmax_full * (grad_probs - weighted_sum)).astype(jnp.bfloat16)  46.6 us
    unnamed x368, local copies, waits for them, and re-layouts  42.4 us
    dot_general x6, matrix products, micro_batch(): jnp.einsum('qhd,khd->hqk', block_grad_out, value_heads, preferred_element...  40.9 us
    concatenate x4, other arithmetic, micro_batch(): attended_heads = jnp.concatenate(mixed_blocks, axis=0).astype(jnp.bfloat16)  32.8 us
    dot_general x2, matrix products, micro_batch(): jnp.einsum('rd,fd->rf', cot_low, mlp_full, preferred_element_type=jnp.flo...  29.9 us
    all_to_all x2, waiting for transfers between devices, micro_batch(): lax.all_to_all(grad_stack, 'sp', split_axis=0, concat_axis=2, tiled=True)  29.5 us
  transfers between devices with their start and end apart: 28, of which 11 were waited for; matrix products, arithmetic and copies ran while one was open for 49% of the time, Pallas kernels for 0%

commit v1 on v0

v1 whole, which is shorter than its diff:
```python
import jax
import jax.numpy as jnp
from jax import lax
from jax.sharding import Mesh, PartitionSpec as P

HEADS = 16
HEAD_DIM = 64
norm_epsilon = 1e-05
rotary_base = 160000.0
masked_score = -1e30
BF = jnp.bfloat16
F32 = jnp.float32
SWAP = [(0, 1), (1, 0)]


def mm(a, b, dims=((1,), (0,))):
    return lax.dot_general(a, b, (dims, ((), ())), preferred_element_type=F32)


def swap(x):
    return lax.ppermute(x, "core", SWAP)


def norm_parts(values):
    centre = values - jnp.mean(values, axis=-1, keepdims=True)
    spread = jnp.mean(centre * centre, axis=-1, keepdims=True)
    scale = lax.rsqrt(spread + norm_epsilon)
    return centre * scale, scale


def norm_back(grad, gain, n, scale):
    h = grad * gain
    back = scale * (
        h - jnp.mean(h, axis=-1, keepdims=True) - n * jnp.mean(h * n, axis=-1, keepdims=True)
    )
    return back, jnp.sum(grad * n, axis=0)


def rotary_tables(places):
    exponents = jnp.arange(0, HEAD_DIM, 2).astype(F32) / HEAD_DIM
    inverse_freq = 1.0 / rotary_base**exponents
    angles = places.astype(F32)[:, None] * inverse_freq[None, :]
    angles = jnp.concatenate([angles, angles], axis=-1)
    return jnp.cos(angles), jnp.sin(angles)


def turn(u):
    half = HEAD_DIM // 2
    return jnp.concatenate([-u[..., half:], u[..., :half]], axis=-1)


def turn_back(u):
    half = HEAD_DIM // 2
    return jnp.concatenate([u[..., half:], -u[..., :half]], axis=-1)


def sequence_layout(lengths_row, positions):
    seq_ends = jnp.cumsum(lengths_row)
    passed = (positions[:, None] >= seq_ends[None, :]).astype(jnp.int32)
    seq_ids = jnp.sum(passed, axis=1)
    seq_starts = jnp.sum(passed * lengths_row[None, :], axis=1)
    return seq_ids, positions - seq_starts


def attend(q, k, v, seq_ids):
    rows, heads = q.shape[0], q.shape[1]
    same = seq_ids[:, None] == seq_ids[None, :]
    out, lse = [], []
    for at in range(0, rows, 512):
        raw = jnp.einsum("qhd,khd->hqk", q[at : at + 512], k, preferred_element_type=F32) * 0.125
        masked = jnp.where(same[at : at + 512][None], raw, masked_score)
        top = jnp.max(masked, axis=-1, keepdims=True)
        terms = jnp.exp(masked - top)
        total = jnp.sum(terms, axis=-1, keepdims=True)
        low = (terms / total).astype(BF)
        out.append(jnp.einsum("hqk,khd->qhd", low, v, preferred_element_type=F32))
        lse.append(top + jnp.log(total))
    return jnp.concatenate(out, 0).astype(BF).reshape(rows, -1), jnp.concatenate(lse, 1)


def attend_back(q, k, v, lse, grad_out, seq_ids):
    rows = q.shape[0]
    same = seq_ids[:, None] == seq_ids[None, :]
    gq, gk, gv = [], 0.0, 0.0
    for at in range(0, rows, 512):
        cut = slice(at, at + 512)
        raw = jnp.einsum("qhd,khd->hqk", q[cut], k, preferred_element_type=F32) * 0.125
        masked = jnp.where(same[cut][None], raw, masked_score)
        probs = jnp.exp(masked - lse[:, cut])
        gv = gv + jnp.einsum(
            "hqk,qhd->khd", probs.astype(BF), grad_out[cut], preferred_element_type=F32
        )
        gp = jnp.einsum("qhd,khd->hqk", grad_out[cut], v, preferred_element_type=F32)
        gs = (probs * (gp - jnp.sum(probs * gp, axis=-1, keepdims=True))).astype(BF)
        gq.append(jnp.einsum("hqk,khd->qhd", gs, k, preferred_element_type=F32) * 0.125)
        gk = gk + jnp.einsum("hqk,qhd->khd", gs, q[cut], preferred_element_type=F32) * 0.125
    return jnp.concatenate(gq, 0).astype(BF), gk.astype(BF), gv.astype(BF)


def on_device(
    tokens,
    cotangent,
    destination,
    seq_lengths,
    qkv_weight,
    output_weight,
    input_weight,
    mlp_weight,
    first_gain,
    second_gain,
):
    sp_count, q_count = lax.axis_size("sp"), lax.axis_size("q")
    s, c = lax.axis_index("sp"), lax.axis_index("core")
    batches, _, block, width = tokens.shape
    groups = 2 * q_count
    each = block // groups
    shard = qkv_weight.shape[0]
    part = 2 * shard // sp_count
    half_ff = mlp_weight.shape[0] // 2
    half_width = width // 2
    rows = 2 * block

    owner = s // (sp_count // 2)
    first_row = (s % (sp_count // 2)) * part

    def piece(k):
        def rows_of(w):
            return lax.dynamic_slice_in_dim(w, first_row, part, 0)

        def cols(w, parts):
            w = rows_of(w).reshape(part, parts, 2, -1)
            return lax.dynamic_index_in_dim(w, k, 2, keepdims=False).reshape(part, -1)

        return (
            cols(qkv_weight, 3),
            cols(output_weight, 1),
            cols(input_weight, 2),
            cols(mlp_weight.T, 1),
        )

    mine, theirs = piece(c), piece(1 - c)
    is_owner = c == owner
    gathered = []
    for a, b in zip(mine, theirs):
        part_w = jnp.where(is_owner, a, swap(b))
        gathered.append(lax.all_gather(part_w, ("q", "sp"), axis=0, tiled=True))
    w_qkv, w_out_half, w_in, w_mlp = gathered
    w_gate, w_up = w_in[:, :half_ff], w_in[:, half_ff:]
    w_out_other = swap(w_out_half)
    w_out = jnp.where(
        c == 0,
        jnp.concatenate([w_out_half, w_out_other], 1),
        jnp.concatenate([w_out_other, w_out_half], 1),
    )
    w_out_rows = w_out.reshape(2, half_width, width)
    w_out_own = lax.dynamic_index_in_dim(w_out_rows, c, 0, keepdims=False)
    w_out_far = lax.dynamic_index_in_dim(w_out_rows, 1 - c, 0, keepdims=False)
    gains = lax.all_gather(
        jnp.stack([first_gain, second_gain]), ("q", "core"), axis=1, tiled=True
    ).astype(F32)
    gain_one, gain_two = gains[0], gains[1]

    dest = destination[:, 0]
    group_of, slot_of = dest // block, dest % block
    idx = jnp.arange(block, dtype=jnp.int32)
    before = (group_of[:, :, None] == group_of[:, None, :]) & (idx[None, None, :] < idx[None, :, None])
    place = group_of * each + jnp.sum(before.astype(jnp.int32), axis=-1)
    picks = idx[None, :, None] == place[:, None, :]
    sort_low = picks.astype(BF)
    slots = jnp.sum(jnp.where(picks, slot_of[:, None, :], 0), axis=-1)
    all_slots = lax.all_gather(slots, ("sp", "q", "core"), axis=0)
    all_slots = all_slots.reshape(sp_count, groups, batches, groups, each)
    my_batch, my_pair = s // 2, s % 2
    my_group = 2 * lax.axis_index("q") + my_pair
    my_slots = lax.dynamic_index_in_dim(all_slots, my_batch, 2, keepdims=False)
    my_slots = lax.dynamic_index_in_dim(my_slots, my_group, 2, keepdims=False)
    my_slots = my_slots.reshape(2, 2, q_count, 2, each).transpose(0, 1, 3, 2, 4)
    my_slots = lax.dynamic_index_in_dim(my_slots, c, 0, keepdims=False).reshape(2, block)
    place_low = (idx[None, :, None] == my_slots[:, None, :]).astype(BF)

    def deal(x):
        srt = jnp.einsum("bij,bjd->bid", sort_low, x[:, 0], preferred_element_type=F32).astype(BF)
        srt = srt.reshape(batches, q_count, 2, each, width).transpose(1, 0, 2, 3, 4)
        srt = srt.reshape(q_count, sp_count, each, width)
        got = lax.all_to_all(srt, "q", 0, 0, tiled=True)
        got = lax.all_to_all(got, "sp", 1, 0, tiled=True)
        got = got.reshape(2, 2, q_count, each, width)
        own = lax.dynamic_index_in_dim(got, c, 0, keepdims=False)
        far = swap(lax.dynamic_index_in_dim(got, 1 - c, 0, keepdims=False))
        both = jnp.stack([jnp.where(c == 0, own, far), jnp.where(c == 0, far, own)], axis=1)
        both = both.reshape(2, block, width)
        return jnp.einsum("tri,tid->trd", place_low, both, preferred_element_type=F32).reshape(
            rows, width
        )

    def give_back(x):
        x = x.reshape(2, block, width)
        x = jnp.einsum("tri,trd->tid", place_low, x, preferred_element_type=F32).astype(BF)
        x = x.reshape(2, 2, q_count, each, width)
        own = lax.dynamic_index_in_dim(x, c, 1, keepdims=False)
        far = swap(lax.dynamic_index_in_dim(x, 1 - c, 1, keepdims=False))
        both = jnp.where(c == 0, jnp.stack([own, far]), jnp.stack([far, own]))
        both = both.reshape(sp_count, q_count, each, width)
        got = lax.all_to_all(both, "sp", 0, 0, tiled=True)
        got = got.reshape(sp_count, q_count, each, width).transpose(1, 0, 2, 3)
        got = lax.all_to_all(got, "q", 0, 0, tiled=True)
        got = got.reshape(q_count, batches, 2, each, width).transpose(1, 0, 2, 3, 4)
        got = got.reshape(batches, block, width)
        out = jnp.einsum("bij,bid->bjd", sort_low, got, preferred_element_type=F32)
        return out.astype(BF)[:, None]

    lengths_row = lax.dynamic_index_in_dim(seq_lengths[:, 0], my_batch, 0, keepdims=False)
    my_lengths = lax.all_gather(seq_lengths[:, 0], "core", axis=0)
    my_lengths = lax.dynamic_index_in_dim(my_lengths, my_pair, 0, keepdims=False)
    lengths_row = lax.dynamic_index_in_dim(my_lengths, my_batch, 0, keepdims=False)

    owned = deal(tokens)
    cot = deal(cotangent).astype(BF)
    positions = (c * rows + jnp.arange(2 * rows, dtype=jnp.int32)) % (2 * rows)
    seq_ids, places = sequence_layout(lengths_row, positions)
    cosine, sine = rotary_tables(places)
    cosine, sine = cosine[:, None, None], sine[:, None, None]

    norm_one, scale_one = norm_parts(owned)
    low_one = (norm_one * gain_one).astype(BF)
    low_one = jnp.concatenate([low_one, swap(low_one)], 0)
    projected = mm(low_one, w_qkv).reshape(2 * rows, 3, HEADS // 2, HEAD_DIM)
    pair = projected[:, :2]
    pair = (pair * cosine + turn(pair) * sine).astype(BF)
    q, k, v = pair[:, 0], pair[:, 1], projected[:, 2].astype(BF)
    att, lse = attend(q, k, v, seq_ids)
    att_own, att_far = att[:rows], swap(att[rows:])
    middle = owned + (mm(att_own, w_out_own) + mm(att_far, w_out_far))
    norm_two, scale_two = norm_parts(middle)
    low_two = (norm_two * gain_two).astype(BF)
    low_two = jnp.concatenate([low_two, swap(low_two)], 0)
    cot_all = jnp.concatenate([cot, swap(cot)], 0)
    gate, up = mm(low_two, w_gate), mm(low_two, w_up)
    phi = 0.5 * (1.0 + lax.erf(gate * (0.5**0.5)))
    act = gate * phi
    hidden = (act * up).astype(BF)
    partial = mm(hidden, w_mlp, ((1,), (1,)))
    result = middle + (partial[:rows] + swap(partial[rows:].astype(BF)))
    layer_output = give_back(result.astype(BF))

    grad_hidden = mm(cot_all, w_mlp)
    slope = phi + gate * (jnp.exp(-0.5 * gate * gate) * (2.0 * jnp.pi) ** -0.5)
    grad_gate = (grad_hidden * up * slope).astype(BF)
    grad_up = (grad_hidden * act).astype(BF)
    d_mlp = mm(cot_all, hidden, ((0,), (0,))).astype(BF)
    d_gate = mm(low_two, grad_gate, ((0,), (0,))).astype(BF)
    d_up = mm(low_two, grad_up, ((0,), (0,))).astype(BF)
    partial = mm(grad_gate, w_gate, ((1,), (1,))) + mm(grad_up, w_up, ((1,), (1,)))
    grad_two = partial[:rows] + swap(partial[rows:].astype(BF))
    back, gain_two_grad = norm_back(grad_two, gain_two, norm_two, scale_two)
    grad_middle = cot.astype(F32) + back
    branch = grad_middle.astype(BF)
    d_out_own = mm(att_own, branch, ((0,), (0,)))
    d_out_far = mm(att_far, branch, ((0,), (0,)))
    d_out = jnp.where(
        c == 0, jnp.concatenate([d_out_own, d_out_far]), jnp.concatenate([d_out_far, d_out_own])
    ).reshape(width, 2, half_width)
    d_out_mine = lax.dynamic_index_in_dim(d_out, c, 1, keepdims=False)
    d_out_theirs = lax.dynamic_index_in_dim(d_out, 1 - c, 1, keepdims=False)
    d_out = (d_out_mine + swap(d_out_theirs.astype(BF))).astype(BF)
    ga_own = mm(branch, w_out_own, ((1,), (1,))).astype(BF)
    ga_far = swap(mm(branch, w_out_far, ((1,), (1,))).astype(BF))
    grad_att = jnp.concatenate([ga_own, ga_far], 0).reshape(2 * rows, HEADS // 2, HEAD_DIM)
    gq, gk, gv = attend_back(q, k, v, lse, grad_att, seq_ids)
    gpair = jnp.stack([gq, gk], axis=1).astype(F32)
    gpair = gpair * cosine + turn_back(gpair * sine)
    grad_proj = jnp.concatenate([gpair.astype(BF), gv[:, None]], axis=1).reshape(2 * rows, -1)
    d_qkv = mm(low_one, grad_proj, ((0,), (0,))).astype(BF)
    partial = mm(grad_proj, w_qkv, ((1,), (1,)))
    grad_one = partial[:rows] + swap(partial[rows:].astype(BF))
    back, gain_one_grad = norm_back(grad_one, gain_one, norm_one, scale_one)
    input_grad = give_back((grad_middle + back).astype(BF))

    def reduce(d):
        d = lax.psum_scatter(d, ("q", "sp"), scatter_dimension=0, tiled=True)
        d = lax.all_gather(d, "sp", axis=0, tiled=True).reshape(2, shard, -1)
        own = lax.dynamic_index_in_dim(d, c, 0, keepdims=False)
        far = swap(lax.dynamic_index_in_dim(d, 1 - c, 0, keepdims=False))
        return own, far

    def joined(d, parts):
        own, far = (x.astype(F32).reshape(shard, parts, 1, -1) for x in reduce(d))
        both = jnp.where(
            c == 0, jnp.concatenate([own, far], 2), jnp.concatenate([far, own], 2)
        )
        return both.reshape(shard, -1)

    mlp_grad = joined(d_mlp, 1).T
    input_grad_w = jnp.concatenate([joined(d_gate, 1), joined(d_up, 1)], 1)
    out_grad = joined(d_out, 1)
    qkv_grad = joined(d_qkv, 3)
    gain_grads = lax.psum(jnp.stack([gain_one_grad, gain_two_grad]), ("sp", "q", "core"))
    at = (2 * lax.axis_index("q") + c) * shard
    gain_grads = lax.dynamic_slice_in_dim(gain_grads, at, shard, 1)
    return (
        layer_output,
        input_grad,
        qkv_grad,
        out_grad,
        input_grad_w,
        mlp_grad,
        gain_grads[0],
        gain_grads[1],
    )


def solution(mesh):
    sp_count, fsdp_count = mesh.devices.shape
    split = Mesh(mesh.devices.reshape(sp_count, fsdp_count // 2, 2), ("sp", "q", "core"))
    fsdp = ("q", "core")
    big = P(None, fsdp, "sp", None)
    return jax.shard_map(
        on_device,
        mesh=split,
        in_specs=(
            big,
            big,
            P(None, fsdp, "sp"),
            P(None, fsdp, None),
            P(fsdp, None),
            P(fsdp, None),
            P(fsdp, None),
            P(None, fsdp),
            P(fsdp),
            P(fsdp),
        ),
        out_specs=(
            big,
            big,
            P(fsdp, None),
            P(fsdp, None),
            P(fsdp, None),
            P(None, fsdp),
            P(fsdp),
            P(fsdp),
        ),
        check_vma=False,
    )
```

time: 1180 us -> 980 us (0.83)
  waiting for transfers between devices: 324 us -> 114 us
  blocking collectives: 49.8 us -> 214 us
  local copies, waits for them, and re-layouts: 175 us -> 74.6 us
  starting transfers between devices: 79.4 us -> 40.7 us
  other arithmetic: 207 us -> 172 us
  matrix products: 318 us -> 336 us
    reduce_scatter x5, waiting for transfers between devices: 162 us -> 9.03 us  [reduce(): d = lax.psum_scatter(d, ('q', 'sp'), scatter_dimension=0, tiled=True)]
    all_gather x2 -> x8, blocking collectives: 22.2 us -> 168 us  [the longest x5 77.4 us: reduce(): d = lax.all_gather(d, 'sp', axis=0, tiled=True).reshape(2, shard, -1)]
    all_to_all x18 -> x8, waiting for transfers between devices: 158 us -> 98.6 us  [the longest x2 32.6 us: give_back(): got = lax.all_to_all(got, 'q', 0, 0, tiled=True)]
    gather x18 -> x0, local copies, waits for them, and re-layouts: 46.3 us -> none  [the longest x4 10.8 us: micro_batch(): returned = (result_low[slot_rows], grad_owned[slot_rows])]
    all_to_all x18 -> x8, starting transfers between devices: 79.1 us -> 33.8 us  [the longest x2 10.7 us: deal(): got = lax.all_to_all(srt, 'q', 0, 0, tiled=True)]
    psum x1, blocking collectives: 10.3 us -> 45.6 us  [on_device(): lax.psum(jnp.stack([gain_one_grad, gain_two_grad]), ('sp', 'q', 'core'))]
    concatenate x11 -> x8, other arithmetic: 37.2 us -> 6.46 us  [the longest x4 2.88 us: joined(): jnp.concatenate([own, far], 2)]
    sort x6 -> x0, other arithmetic: 22.6 us -> none  [the longest x2 7.54 us: micro_batch(): placing = jnp.argsort(slot_rows)]
  transfers between devices with their start and end apart: 28 -> 40, of which waited for: 11 -> 10; matrix products, arithmetic and copies ran while one was open for 49% -> 52% of each run, Pallas kernels for 0% -> 0%
where the time goes in v1:
time: 980 us; the launch traced here: 967 us
  matrix products  336 us (34%)
  blocking collectives  214 us (22%)
  other arithmetic  172 us (18%)
  waiting for transfers between devices  114 us (12%)
  local copies, waits for them, and re-layouts  74.6 us (8%)
  starting transfers between devices  40.7 us (4%)
  between operations  15.7 us (2%)
    dot_general x18, matrix products, mm(): return lax.dot_general(a, b, (dims, ((), ())), preferred_element_type=F32)  119 us
    all_gather x5, blocking collectives, reduce(): d = lax.all_gather(d, 'sp', axis=0, tiled=True).reshape(2, shard, -1)  77.4 us
    convert_element_type x3, other arithmetic, attend_back(): gs = (probs * (gp - jnp.sum(probs * gp, axis=-1, keepdims=True))).astype(BF)  66.7 us
    dot_general x3, matrix products, attend_back(): jnp.einsum('qhd,khd->hqk', grad_out[cut], v, preferred_element_type=F32)  50.7 us
    all_gather x1, blocking collectives, on_device(): lax.all_gather(jnp.stack([first_gain, second_gain]), ('q', 'core'), axis=...  47 us
    psum x1, blocking collectives, on_device(): lax.psum(jnp.stack([gain_one_grad, gain_two_grad]), ('sp', 'q', 'core'))  45.6 us
    all_gather x1, blocking collectives, on_device(): all_slots = lax.all_gather(slots, ('sp', 'q', 'core'), axis=0)  41.9 us
    dot_general x3, matrix products, attend_back(): jnp.einsum('hqk,qhd->khd', probs.astype(BF), grad_out[cut], preferred_ele...  39.8 us
  transfers between devices with their start and end apart: 40, of which 10 were waited for; matrix products, arithmetic and copies ran while one was open for 52% of the time, Pallas kernels for 0%

profile of v1, /device:TPU:0, one launch (start us, length us, event | category | flops | bytes accessed | tf_op | source)
XLA Modules:
  0.0 967.3 jit_solution(8671832579128092968)
XLA Ops:
  45.3 21.7 %all-to-all-done = bf16[4,4,48,1024]{3,2,1,0:T(8,128)(2,1)S(1)} async-done(((bf16[4,4,48,1024]{3,2,1,0:T(8,128)(2,1)}), bf16[4,4,48,1024]{3,2,1,0:T(8,128)(2,1)S(1)}, u32[]{:S(2)}, u32[]{:S(2)}) %all-to-all-start) | async-done | bytes 1572896 | tf_op jit(solution)/shard_map/all_to_all | solution.py:185
  74.0 41.9 %all-gather.2 = s32[32,2,384]{2,1,0:T(2,128)S(1)} all-gather(s32[1,2,384]{2,1,0:T(2,128)S(1)} %bitcast.426), channel_id=2, replica_groups=mesh['sp'=4,'q'=4,'core'=2] {'sp','q','core'}, dimensions={0}, use_global_device_ids=true | all-gather | bytes 101376 | tf_op jit(solution)/shard_map/all_gather | solution.py:171
  127.6 47.0 %all_gather.41 = bf16[2,1024]{1,0:T(2,128)(2,1)S(1)} all-gather(bf16[2,128]{1,0:T(2,128)(2,1)S(1)} %pad_maximum_fusion.17), channel_id=1, replica_groups=mesh['sp'=4,'q'=4,'core'=2] {'q','core'}, dimensions={1}, use_global_device_ids=true | all-gather | bytes 4608 | tf_op jit(solution)/shard_map/all_gather | solution.py:158
  199.5 18.4 %all-to-all-done.5 = bf16[4,4,48,1024]{3,2,0,1:T(8,128)(2,1)} async-done(((bf16[4,4,48,1024]{3,2,0,1:T(8,128)(2,1)}), bf16[4,4,48,1024]{3,2,0,1:T(8,128)(2,1)}, u32[]{:S(2)}, u32[]{:S(2)}) %all-to-all-start.5) | async-done | bytes 1572896 | tf_op jit(solution)/shard_map/all_to_all | solution.py:186
  234.1 11.0 %fusion.126 = (f32[8,512]{1,0:T(8,128)S(1)}, f32[8,512,1536]{2,1,0:T(8,128)}) fusion(bf16[1536,2,8,64]{0,3,2,1:T(8,128)(2,1)S(1)} %fusion.27, pred[512,1536]{1,0:T(8,128)(4,1)S(1)} %get-tuple-element.76), kind=kOutput, calls=%fused_computation.294 | convolution fusion | flops 824176640 | bytes 28065792 | tf_op jit(solution)/shard_map/qhd,khd->hqk/dot_general | solution.py:70
  245.1 11.3 %fusion.1 = f32[8,512]{1,0:T(8,128)S(1)} fusion(f32[8,512,1536]{2,1,0:T(8,128)} %get-tuple-element.115, f32[8,512]{1,0:T(8,128)S(1)} %get-tuple-element.114), kind=kLoop, calls=%fused_computation.19 | loop fusion | flops 12578816 | bytes 25198592 | tf_op jit(solution)/shard_map/reduce_sum | solution.py:74
  256.3 11.8 %fusion.71 = bf16[512,8,64]{0,2,1:T(8,128)(2,1)S(1)} fusion(f32[8,512,1536]{2,1,0:T(8,128)} %get-tuple-element.115, f32[8,512]{1,0:T(8,128)S(1)} %fusion.1, f32[8,512]{1,0:T(8,128)S(1)} %get-tuple-element.114, f32[1536,3,8,64]{0,3,2,1:T(8,128)} %bitcast.356), kind=kOutput, calls=%fused_computation.151 | convolution fusion | flops 824442880 | bytes 27295744 | tf_op jit(solution)/shard_map/hqk,khd->qhd/dot_general | solution.py:76
  268.2 11.1 %fusion.128 = (f32[8,512]{1,0:T(8,128)S(1)}, f32[8,512,1536]{2,1,0:T(8,128)}) fusion(bf16[1536,2,8,64]{0,3,2,1:T(8,128)(2,1)S(1)} %fusion.27, pred[512,1536]{1,0:T(8,128)(4,1)S(1)} %get-tuple-element.75), kind=kOutput, calls=%fused_computation.296 | convolution fusion | flops 824176640 | bytes 28065792 | tf_op jit(solution)/shard_map/qhd,khd->hqk/dot_general | solution.py:70
  279.3 11.3 %fusion.2 = f32[8,512]{1,0:T(8,128)S(1)} fusion(f32[8,512,1536]{2,1,0:T(8,128)} %get-tuple-element.119, f32[8,512]{1,0:T(8,128)S(1)} %get-tuple-element.118), kind=kLoop, calls=%fused_computation.20 | loop fusion | flops 12578816 | bytes 25198592 | tf_op jit(solution)/shard_map/reduce_sum | solution.py:74
  290.6 11.5 %fusion.72 = bf16[512,8,64]{0,2,1:T(8,128)(2,1)S(1)} fusion(f32[8,512,1536]{2,1,0:T(8,128)} %get-tuple-element.119, f32[8,512]{1,0:T(8,128)S(1)} %fusion.2, f32[8,512]{1,0:T(8,128)S(1)} %get-tuple-element.118, f32[1536,3,8,64]{0,3,2,1:T(8,128)} %bitcast.357), kind=kOutput, calls=%fused_computation.152 | convolution fusion | flops 824442880 | bytes 27295744 | tf_op jit(solution)/shard_map/hqk,khd->qhd/dot_general | solution.py:76
  302.2 10.9 %fusion.127 = (f32[8,512]{1,0:T(8,128)S(1)}, f32[8,512,1536]{2,1,0:T(8,128)}) fusion(bf16[1536,2,8,64]{0,3,2,1:T(8,128)(2,1)S(1)} %fusion.27, pred[512,1536]{1,0:T(8,128)(4,1)S(1)} %get-tuple-element.74), kind=kOutput, calls=%fused_computation.295 | convolution fusion | flops 824176640 | bytes 28065792 | tf_op jit(solution)/shard_map/qhd,khd->hqk/dot_general | solution.py:70
  313.1 11.3 %fusion = f32[8,512]{1,0:T(8,128)S(1)} fusion(f32[8,512,1536]{2,1,0:T(8,128)} %get-tuple-element.117, f32[8,512]{1,0:T(8,128)S(1)} %get-tuple-element.116), kind=kLoop, calls=%fused_computation.18 | loop fusion | flops 12578816 | bytes 25198592 | tf_op jit(solution)/shard_map/reduce_sum | solution.py:74
  324.4 12.0 %fusion.70 = bf16[512,8,64]{0,2,1:T(8,128)(2,1)S(1)} fusion(f32[8,512,1536]{2,1,0:T(8,128)} %get-tuple-element.117, f32[8,512]{1,0:T(8,128)S(1)} %fusion, f32[8,512]{1,0:T(8,128)S(1)} %get-tuple-element.116, f32[1536,3,8,64]{0,3,2,1:T(8,128)} %bitcast.358), kind=kOutput, calls=%fused_computation.150 | convolution fusion | flops 824442880 | bytes 27295744 | tf_op jit(solution)/shard_map/hqk,khd->qhd/dot_general | solution.py:76
  349.5 10.1 %fusion.54 = f32[1536,1312]{0,1:T(8,128)} fusion(bf16[1024,1312]{1,0:T(8,128)(2,1)} %all-gather.14.cloned.1.call-done, bf16[768,1024]{1,0:T(8,128)(2,1)} %collective-permute-done.12, bf16[768,1024]{1,0:T(8,128)(2,1)S(1)} %bitcast.364), kind=kOutput, calls=%fused_computation.111 | convolution fusion | flops 4133486592 | bytes 13893632 | tf_op jit(solution)/shard_map/dot_general | solution.py:17
  359.6 10.5 %fusion.48 = f32[1536,1312]{0,1:T(8,128)} fusion(bf16[1024,2624]{1,0:T(8,128)(2,1)} %all-gather.12.cloned.1.call-done, bf16[768,1024]{1,0:T(8,128)(2,1)} %collective-permute-done.6, bf16[768,1024]{1,0:T(8,128)(2,1)S(1)} %multiply_convert_fusion.5), kind=kOutput, calls=%fused_computation.102 | convolution fusion | flops 4133486592 | bytes 14090240 | tf_op jit(solution)/shard_map/dot_general | solution.py:17
  370.1 16.6 %fusion.23 = (bf16[1536,1312]{0,1:T(8,128)(2,1)}, bf16[1536,1312]{0,1:T(8,128)(2,1)}, bf16[1536,1312]{0,1:T(8,128)(2,1)}) fusion(f32[1536,1312]{0,1:T(8,128)} %fusion.54, f32[1536,1312]{0,1:T(8,128)} %fusion.48, bf16[1024,2624]{1,0:T(8,128)(2,1)} %all-gather.12.cloned.1.call-done, bf16[768,1024]{1,0:T(8,128)(2,1)} %collective-permute-done.6, ...), kind=kOutput, calls=%fused_computation.39 | convolution fusion | flops 4165730304 | bytes 34242560 | tf_op jit(solution)/shard_map/dot_general | solution.py:17
  465.2 12.3 %fusion.6 = f32[8,64,1536]{2,1,0:T(8,128)} fusion(bf16[512,8,64]{0,2,1:T(8,128)(2,1)S(1)} %bitcast.385, f32[8,512,1536]{2,1,0:T(8,128)} %get-tuple-element.119, f32[8,512]{1,0:T(8,128)S(1)} %log_add_fusion), kind=kOutput, calls=%fused_computation.24 | convolution fusion | flops 817889280 | bytes 28852224 | tf_op jit(solution)/shard_map/hqk,qhd->khd/dot_general | solution.py:90
  477.6 16.7 %multiply_reduce_fusion = (f32[8,512]{1,0:T(8,128)S(1)}, f32[8,512,1536]{2,1,0:T(8,128)}) fusion(f32[8,512,1536]{2,1,0:T(8,128)} %get-tuple-element.119, f32[8,512]{1,0:T(8,128)S(1)} %log_add_fusion, bf16[512,8,64]{0,2,1:T(8,128)(2,1)S(1)} %bitcast.386, f32[1536,3,8,64]{0,3,2,1:T(8,128)} %bitcast.359), kind=kOutput, calls=%fused_computation.1 | convolution fusion | flops 824176640 | bytes 52461568 | tf_op jit(solution)/shard_map/qhd,khd->hqk/dot_general | solution.py:93
  494.3 12.0 %fusion.10 = f32[8,64,1536]{2,1,0:T(8,128)} fusion(bf16[512,8,64]{0,2,1:T(8,128)(2,1)S(1)} %bitcast.383, f32[8,512,1536]{2,1,0:T(8,128)} %get-tuple-element.117, f32[8,512]{1,0:T(8,128)S(1)} %log_add_fusion.2), kind=kOutput, calls=%fused_computation.26 | convolution fusion | flops 817889280 | bytes 28852224 | tf_op jit(solution)/shard_map/hqk,qhd->khd/dot_general | solution.py:90
  506.3 17.1 %multiply_reduce_fusion.2 = (f32[8,512]{1,0:T(8,128)S(1)}, f32[8,512,1536]{2,1,0:T(8,128)}) fusion(f32[8,512,1536]{2,1,0:T(8,128)} %get-tuple-element.117, f32[8,512]{1,0:T(8,128)S(1)} %log_add_fusion.2, bf16[512,8,64]{0,2,1:T(8,128)(2,1)S(1)} %bitcast.384, f32[1536,3,8,64]{0,3,2,1:T(8,128)} %bitcast.360), kind=kOutput, calls=%fused_computation.7 | convolution fusion | flops 824176640 | bytes 52461568 | tf_op jit(solution)/shard_map/qhd,khd->hqk/dot_general | solution.py:93
  523.4 22.1 %multiply_convert_fusion.2 = bf16[8,512,1536]{2,1,0:T(8,128)(2,1)} fusion(f32[8,512,1536]{2,1,0:T(8,128)} %get-tuple-element.123, f32[8,512,1536]{2,1,0:T(8,128)} %get-tuple-element.117, f32[8,512]{1,0:T(8,128)S(1)} %get-tuple-element.122, f32[8,512]{1,0:T(8,128)S(1)} %log_add_fusion.2), kind=kLoop, calls=%fused_computation.6 | loop fusion | flops 25165824 | bytes 62947328 | tf_op jit(solution)/shard_map/convert_element_type | solution.py:94
  562.6 16.8 %multiply_reduce_fusion.1 = (f32[8,512]{1,0:T(8,128)S(1)}, f32[8,512,1536]{2,1,0:T(8,128)}) fusion(f32[8,512,1536]{2,1,0:T(8,128)} %get-tuple-element.115, f32[8,512]{1,0:T(8,128)S(1)} %log_add_fusion.1, bf16[512,8,64]{0,2,1:T(8,128)(2,1)S(1)} %bitcast.391, f32[1536,3,8,64]{0,3,2,1:T(8,128)} %bitcast.361), kind=kOutput, calls=%fused_computation.4 | convolution fusion | flops 824176640 | bytes 52461568 | tf_op jit(solution)/shard_map/qhd,khd->hqk/dot_general | solution.py:93
  579.5 22.2 %multiply_convert_fusion.1 = bf16[8,512,1536]{2,1,0:T(8,128)(2,1)} fusion(f32[8,512,1536]{2,1,0:T(8,128)} %get-tuple-element.125, f32[8,512,1536]{2,1,0:T(8,128)} %get-tuple-element.115, f32[8,512]{1,0:T(8,128)S(1)} %get-tuple-element.124, f32[8,512]{1,0:T(8,128)S(1)} %log_add_fusion.1), kind=kLoop, calls=%fused_computation.3 | loop fusion | flops 25165824 | bytes 62947328 | tf_op jit(solution)/shard_map/convert_element_type | solution.py:94
  610.2 22.4 %multiply_convert_fusion = bf16[8,512,1536]{2,1,0:T(8,128)(2,1)} fusion(f32[8,512,1536]{2,1,0:T(8,128)} %get-tuple-element.127, f32[8,512,1536]{2,1,0:T(8,128)} %get-tuple-element.119, f32[8,512]{1,0:T(8,128)S(1)} %get-tuple-element.126, f32[8,512]{1,0:T(8,128)S(1)} %log_add_fusion), kind=kLoop, calls=%fused_computation | loop fusion | flops 25165824 | bytes 62947328 | tf_op jit(solution)/shard_map/convert_element_type | solution.py:94
  655.4 15.5 %fusion.43 = bf16[1536,1,8,64]{0,3,2,1:T(8,128)(2,1)} fusion(f32[8,64,1536]{2,1,0:T(8,128)} %fusion.6, f32[8,64,1536]{2,1,0:T(8,128)} %fusion.10, bf16[512,8,64]{0,2,1:T(8,128)(2,1)} %bitcast.392, f32[8,512,1536]{2,1,0:T(8,128)} %get-tuple-element.115, f32[8,512]{1,0:T(8,128)S(1)} %log_add_fusion.1), kind=kOutput, calls=%fused_computation.98 | convolution fusion | flops 820248576 | bytes 33570816 | tf_op jit(solution)/shard_map/hqk,qhd->khd/dot_general | solution.py:90
  713.1 25.8 %all-to-all-done.2 = bf16[4,4,48,1024]{3,2,1,0:T(8,128)(2,1)S(1)} async-done(((bf16[4,4,48,1024]{3,2,1,0:T(8,128)(2,1)}), bf16[4,4,48,1024]{3,2,1,0:T(8,128)(2,1)S(1)}, u32[]{:S(2)}, u32[]{:S(2)}) %all-to-all-start.2) | async-done | bytes 1572896 | tf_op jit(solution)/shard_map/all_to_all | solution.py:204
  740.2 45.6 %psum.7 = f32[2,1024]{1,0:T(2,128)S(1)} all-reduce(f32[2,1024]{1,0:T(2,128)S(1)} %pad_maximum_fusion.16), channel_id=1, replica_groups=mesh['sp'=4,'q'=4,'core'=2] {'sp','q','core'}, use_global_device_ids=true, to_apply=%region_29.30 | all-reduce | flops 2048 | bytes 16384 | tf_op jit(solution)/shard_map/psum | solution.py:297
  805.2 28.0 %all_gather.49 = bf16[256,1312]{1,0:T(8,128)(2,1)S(1)} all-gather(bf16[64,1312]{1,0:T(8,128)(2,1)} %reduce-scatter.10.cloned.1.call-done), channel_id=1, replica_groups=mesh['sp'=4,'q'=4,'core'=2] {'sp'}, dimensions={0}, use_global_device_ids=true | all-gather | bytes 839680 | tf_op jit(solution)/shard_map/all_gather | solution.py:281
  834.4 14.7 %all_gather.51 = bf16[256,1312]{1,0:T(8,128)(2,1)} all-gather(bf16[64,1312]{1,0:T(8,128)(2,1)} %reduce-scatter.14.cloned.1.call-done), channel_id=1, replica_groups=mesh['sp'=4,'q'=4,'core'=2] {'sp'}, dimensions={0}, use_global_device_ids=true | all-gather | bytes 839680 | tf_op jit(solution)/shard_map/all_gather | solution.py:281
  849.1 13.4 %all_gather.50 = bf16[256,1312]{1,0:T(8,128)(2,1)} all-gather(bf16[64,1312]{1,0:T(8,128)(2,1)} %reduce-scatter.12.cloned.1.call-done), channel_id=1, replica_groups=mesh['sp'=4,'q'=4,'core'=2] {'sp'}, dimensions={0}, use_global_device_ids=true | all-gather | bytes 839680 | tf_op jit(solution)/shard_map/all_gather | solution.py:281
  884.5 27.1 %all-to-all-done.3 = bf16[4,4,48,1024]{3,2,1,0:T(8,128)(2,1)S(1)} async-done(((bf16[4,4,48,1024]{3,2,1,0:T(8,128)(2,1)}), bf16[4,4,48,1024]{3,2,1,0:T(8,128)(2,1)S(1)}, u32[]{:S(2)}, u32[]{:S(2)}) %all-to-all-start.3) | async-done | bytes 1572896 | tf_op jit(solution)/shard_map/all_to_all | solution.py:206
  935.4 11.2 %all_gather.47 = bf16[256,1536]{1,0:T(8,128)(2,1)S(1)} all-gather(bf16[64,1536]{1,0:T(8,128)(2,1)} %reduce-scatter.6.cloned.1.call-done), channel_id=1, replica_groups=mesh['sp'=4,'q'=4,'core'=2] {'sp'}, dimensions={0}, use_global_device_ids=true | all-gather | bytes 983040 | tf_op jit(solution)/shard_map/all_gather | solution.py:281
  (391 shorter events, 360.2 us)
Async XLA Ops:
  7.2 192.1 %all-gather.10.cloned.1.call-start = ((), (), s32[]{:S(2)}) async-start(), calls=%async_computation.14 | async-start | bytes 1114112 | tf_op jit(solution)/shard_map/all_gather | solution.py:146
  10.8 209.3 %all-gather.8.cloned.1.call-start = ((), (), s32[]{:S(2)}) async-start(), calls=%async_computation.13 | async-start | bytes 3342336 | tf_op jit(solution)/shard_map/all_gather | solution.py:146
  20.0 47.1 %all-to-all-start = ((bf16[4,4,48,1024]{3,2,1,0:T(8,128)(2,1)}), bf16[4,4,48,1024]{3,2,1,0:T(8,128)(2,1)S(1)}, u32[]{:S(2)}, u32[]{:S(2)}) async-start(bf16[4,4,48,1024]{3,2,1,0:T(8,128)(2,1)} %bitcast.12), calls=%async_computation | async-start | bytes 3145728 | tf_op jit(solution)/shard_map/all_to_all | solution.py:185
  34.5 162.7 %collective-permute-start.7 = (bf16[64,2624]{1,0:T(8,128)(2,1)}, bf16[64,2624]{1,0:T(8,128)(2,1)}, u32[]{:S(2)}, u32[]{:S(2)}) collective-permute-start(bf16[64,2624]{1,0:T(8,128)(2,1)} %reshape.658), channel_id=1, source_target_pairs={{0,1},{1,0},{2,3},{3,2},{4,5},{5,4},{6,7},{7,6},{8,9},{9,8},{10,11... | collective-permute-start | bytes 1007624 | tf_op jit(solution)/shard_map/ppermute | solution.py:21
  36.7 36.2 %collective-permute-start.8 = (bf16[64,1312]{1,0:T(8,128)(2,1)}, bf16[64,1312]{1,0:T(8,128)(2,1)}, u32[]{:S(2)}, u32[]{:S(2)}) collective-permute-start(bf16[64,1312]{1,0:T(8,128)(2,1)} %bitcast.52), channel_id=1, source_target_pairs={{0,1},{1,0},{2,3},{3,2},{4,5},{5,4},{6,7},{7,6},{8,9},{9,8},{10,11... | collective-permute-start | bytes 503816 | tf_op jit(solution)/shard_map/ppermute | solution.py:21
  68.4 52.1 %all-to-all-start.1 = ((bf16[4,4,48,1024]{3,2,0,1:T(8,128)(2,1)}), bf16[4,4,48,1024]{3,2,0,1:T(8,128)(2,1)}, u32[]{:S(2)}, u32[]{:S(2)}) async-start(bf16[4,4,48,1024]{3,2,0,1:T(8,128)(2,1)} %copy.176), calls=%async_computation.1 | async-start | bytes 3145728 | tf_op jit(solution)/shard_map/all_to_all | solution.py:186
  72.9 276.6 %all-gather.14.cloned.1.call-start = ((), (), s32[]{:S(2)}) async-start(), calls=%async_computation.16 | async-start | bytes 3063808 | tf_op jit(solution)/shard_map/all_gather | solution.py:146
  120.5 65.3 %all-to-all-start.4 = ((bf16[4,4,48,1024]{3,2,1,0:T(8,128)(2,1)}), bf16[4,4,48,1024]{3,2,1,0:T(8,128)(2,1)}, u32[]{:S(2)}, u32[]{:S(2)}) async-start(bf16[4,4,48,1024]{3,2,1,0:T(8,128)(2,1)} %bitcast.367), calls=%async_computation.4 | async-start | bytes 3145728 | tf_op jit(solution)/shard_map/all_to_all | solution.py:185
  126.1 49.1 %collective-permute-start = (bf16[2,4,48,1024]{3,2,1,0:T(8,128)(2,1)S(1)}, bf16[2,4,48,1024]{3,2,1,0:T(8,128)(2,1)}, u32[]{:S(2)}, u32[]{:S(2)}) collective-permute-start(bf16[2,4,48,1024]{3,2,1,0:T(8,128)(2,1)S(1)} %dynamic-slice_bitcast_fusion.5), channel_id=1, source_target_pairs={{0,1},{1,0},{2,3},{3,2},{4,5},{5,4},{6,7},{7,6},{8,9},{9,8},{10,11... | collective-permute-start | bytes 2359304 | tf_op jit(solution)/shard_map/ppermute | solution.py:21
  185.5 34.5 %collective-permute-start.1 = (bf16[768,1024]{1,0:T(8,128)(2,1)}, bf16[768,1024]{1,0:T(8,128)(2,1)}, u32[]{:S(2)}, u32[]{:S(2)}) collective-permute-start(bf16[768,1024]{1,0:T(8,128)(2,1)} %multiply_convert_fusion.6), channel_id=1, source_target_pairs={{0,1},{1,0},{2,3},{3,2},{4,5},{5,4},{6,7},{7,6},{8,9},{9,8},{10,11... | collective-permute-start | bytes 4718600 | tf_op jit(solution)/shard_map/ppermute | solution.py:21
  188.6 29.4 %all-to-all-start.5 = ((bf16[4,4,48,1024]{3,2,0,1:T(8,128)(2,1)}), bf16[4,4,48,1024]{3,2,0,1:T(8,128)(2,1)}, u32[]{:S(2)}, u32[]{:S(2)}) async-start(bf16[4,4,48,1024]{3,2,0,1:T(8,128)(2,1)} %copy.187), calls=%async_computation.5 | async-start | bytes 3145728 | tf_op jit(solution)/shard_map/all_to_all | solution.py:186
  193.0 166.7 %all-gather.12.cloned.1.call-start = ((), (), s32[]{:S(2)}) async-start(), calls=%async_computation.15 | async-start | bytes 5849088 | tf_op jit(solution)/shard_map/all_gather | solution.py:146
  199.2 587.2 %reduce-scatter.8.cloned.1.call-start = ((), (), s32[]{:S(2)}) async-start(), calls=%async_computation.18 | async-start | bytes 1114112 | tf_op jit(solution)/shard_map/reduce_scatter | solution.py:280
  199.3 137.7 %collective-permute-start.4 = (bf16[1024,512]{1,0:T(8,128)(2,1)}, bf16[1024,512]{1,0:T(8,128)(2,1)}, u32[]{:S(2)}, u32[]{:S(2)}) collective-permute-start(bf16[1024,512]{1,0:T(8,128)(2,1)} %all-gather.10.cloned.1.call-done), channel_id=1, source_target_pairs={{0,1},{1,0},{2,3},{3,2},{4,5},{5,4},{6,7},{7,6},{8,9},{9,8},{10,11... | collective-permute-start | bytes 3145736 | tf_op jit(solution)/shard_map/ppermute | solution.py:21
  220.0 120.1 %collective-permute-start.11 = (bf16[2,4,48,1024]{3,2,1,0:T(8,128)(2,1)}, bf16[2,4,48,1024]{3,2,1,0:T(8,128)(2,1)}, u32[]{:S(2)}, u32[]{:S(2)}) collective-permute-start(bf16[2,4,48,1024]{3,2,1,0:T(8,128)(2,1)} %dynamic-slice_bitcast_fusion.2), channel_id=1, source_target_pairs={{0,1},{1,0},{2,3},{3,2},{4,5},{5,4},{6,7},{7,6},{8,9},{9,8},{10,11... | collective-permute-start | bytes 2359304 | tf_op jit(solution)/shard_map/ppermute | solution.py:21
  336.6 8.0 collective-permute-start.5
  349.2 10.5 %collective-permute-start.6 = (bf16[768,1024]{1,0:T(8,128)(2,1)S(1)}, bf16[768,1024]{1,0:T(8,128)(2,1)}, u32[]{:S(2)}, u32[]{:S(2)}) collective-permute-start(bf16[768,1024]{1,0:T(8,128)(2,1)S(1)} %multiply_convert_fusion.5), channel_id=1, source_target_pairs={{0,1},{1,0},{2,3},{3,2},{4,5},{5,4},{6,7},{7,6},{8,9},{9,8},{10,11... | collective-permute-start | bytes 4718600 | tf_op jit(solution)/shard_map/ppermute | solution.py:21
  402.2 7.4 collective-permute-start.13
  431.7 373.5 %reduce-scatter.10.cloned.1.call-start = ((), (), s32[]{:S(2)}) async-start(), calls=%async_computation.19 | async-start | bytes 3063808 | tf_op jit(solution)/shard_map/reduce_scatter | solution.py:280
  440.9 393.5 %reduce-scatter.14.cloned.1.call-start = ((), (), s32[]{:S(2)}) async-start(), calls=%async_computation.21 | async-start | bytes 3063808 | tf_op jit(solution)/shard_map/reduce_scatter | solution.py:280
  449.8 399.3 %reduce-scatter.12.cloned.1.call-start = ((), (), s32[]{:S(2)}) async-start(), calls=%async_computation.20 | async-start | bytes 3063808 | tf_op jit(solution)/shard_map/reduce_scatter | solution.py:280
  453.2 10.7 %collective-permute-start.14 = (bf16[768,512]{0,1:T(8,128)(2,1)}, bf16[768,512]{0,1:T(8,128)(2,1)}, u32[]{:S(2)}, u32[]{:S(2)}) collective-permute-start(bf16[768,512]{0,1:T(8,128)(2,1)} %convolution_convert_fusion.11), channel_id=1, source_target_pairs={{0,1},{1,0},{2,3},{3,2},{4,5},{5,4},{6,7},{7,6},{8,9},{9,8},{10,11... | collective-permute-start | bytes 2359304 | tf_op jit(solution)/shard_map/ppermute | solution.py:21
  684.1 11.3 %collective-permute-start.15 = (bf16[768,1024]{1,0:T(8,128)(2,1)}, bf16[768,1024]{1,0:T(8,128)(2,1)S(1)}, u32[]{:S(2)}, u32[]{:S(2)}) collective-permute-start(bf16[768,1024]{1,0:T(8,128)(2,1)} %slice.265), channel_id=1, source_target_pairs={{0,1},{1,0},{2,3},{3,2},{4,5},{5,4},{6,7},{7,6},{8,9},{9,8},{10,11... | collective-permute-start | bytes 4718600 | tf_op jit(solution)/shard_map/ppermute | solution.py:21
  691.8 47.1 %all-to-all-start.2 = ((bf16[4,4,48,1024]{3,2,1,0:T(8,128)(2,1)}), bf16[4,4,48,1024]{3,2,1,0:T(8,128)(2,1)S(1)}, u32[]{:S(2)}, u32[]{:S(2)}) async-start(bf16[4,4,48,1024]{3,2,1,0:T(8,128)(2,1)} %bitcast.58), calls=%async_computation.2 | async-start | bytes 3145728 | tf_op jit(solution)/shard_map/all_to_all | solution.py:204
  695.4 240.0 %reduce-scatter.6.cloned.1.call-start = ((), (), s32[]{:S(2)}) async-start(), calls=%async_computation.17 | async-start | bytes 3342336 | tf_op jit(solution)/shard_map/reduce_scatter | solution.py:280
  704.4 92.2 %collective-permute-start.16 = (bf16[2,4,48,1024]{3,2,1,0:T(8,128)(2,1)S(1)}, bf16[2,4,48,1024]{3,2,1,0:T(8,128)(2,1)}, u32[]{:S(2)}, u32[]{:S(2)}) collective-permute-start(bf16[2,4,48,1024]{3,2,1,0:T(8,128)(2,1)S(1)} %get-tuple-element.80), channel_id=1, source_target_pairs={{0,1},{1,0},{2,3},{3,2},{4,5},{5,4},{6,7},{7,6},{8,9},{9,8},{10,11... | collective-permute-start | bytes 2359304 | tf_op jit(solution)/shard_map/ppermute | solution.py:21
  799.4 64.0 %all-to-all-start.6 = ((bf16[4,4,48,1024]{3,2,1,0:T(8,128)(2,1)}), bf16[4,4,48,1024]{3,2,1,0:T(8,128)(2,1)S(1)}, u32[]{:S(2)}, u32[]{:S(2)}) async-start(bf16[4,4,48,1024]{3,2,1,0:T(8,128)(2,1)} %bitcast.99), calls=%async_computation.6 | async-start | bytes 3145728 | tf_op jit(solution)/shard_map/all_to_all | solution.py:204
  834.4 45.7 %collective-permute-start.20 = (bf16[128,1312]{0,1:T(8,128)(2,1)}, bf16[128,1312]{0,1:T(8,128)(2,1)}, u32[]{:S(2)}, u32[]{:S(2)}) collective-permute-start(bf16[128,1312]{0,1:T(8,128)(2,1)} %bitcast.126), channel_id=1, source_target_pairs={{0,1},{1,0},{2,3},{3,2},{4,5},{5,4},{6,7},{7,6},{8,9},{9,8},{10,11... | collective-permute-start | bytes 1007624 | tf_op jit(solution)/shard_map/ppermute | solution.py:21
  863.4 48.2 %all-to-all-start.3 = ((bf16[4,4,48,1024]{3,2,1,0:T(8,128)(2,1)}), bf16[4,4,48,1024]{3,2,1,0:T(8,128)(2,1)S(1)}, u32[]{:S(2)}, u32[]{:S(2)}) async-start(bf16[4,4,48,1024]{3,2,1,0:T(8,128)(2,1)} %bitcast.352), calls=%async_computation.3 | async-start | bytes 3145728 | tf_op jit(solution)/shard_map/all_to_all | solution.py:206
  875.9 46.6 %collective-permute-start.22 = (bf16[128,1312]{0,1:T(8,128)(2,1)}, bf16[128,1312]{0,1:T(8,128)(2,1)S(1)}, u32[]{:S(2)}, u32[]{:S(2)}) collective-permute-start(bf16[128,1312]{0,1:T(8,128)(2,1)} %bitcast.413), channel_id=1, source_target_pairs={{0,1},{1,0},{2,3},{3,2},{4,5},{5,4},{6,7},{7,6},{8,9},{9,8},{10,11... | collective-permute-start | bytes 1007624 | tf_op jit(solution)/shard_map/ppermute | solution.py:21
  911.6 44.3 %all-to-all-start.7 = ((bf16[4,4,48,1024]{3,2,1,0:T(8,128)(2,1)}), bf16[4,4,48,1024]{3,2,1,0:T(8,128)(2,1)S(1)}, u32[]{:S(2)}, u32[]{:S(2)}) async-start(bf16[4,4,48,1024]{3,2,1,0:T(8,128)(2,1)} %bitcast.370), calls=%async_computation.7 | async-start | bytes 3145728 | tf_op jit(solution)/shard_map/all_to_all | solution.py:206
  946.7 11.8 %collective-permute-start.17 = (bf16[128,1536]{1,0:T(8,128)(2,1)S(1)}, bf16[128,1536]{1,0:T(8,128)(2,1)S(1)}, u32[]{:S(2)}, u32[]{:S(2)}) collective-permute-start(bf16[128,1536]{1,0:T(8,128)(2,1)S(1)} %get-tuple-element.84), channel_id=1, source_target_pairs={{0,1},{1,0},{2,3},{3,2},{4,5},{5,4},{6,7},{7,6},{8,9},{9,8},{10,11... | collective-permute-start | bytes 1179656 | tf_op jit(solution)/shard_map/ppermute | solution.py:21
  (77 other events, 960.4 us)
Sparse Core Ops, SparseCore 0:
  10.9 70.1 all-gather.9
  84.5 88.1 all-gather.7
  175.4 73.3 all-gather.13
  252.0 85.1 all-gather.11
  431.9 85.2 reduce-scatter.7
  519.3 80.1 reduce-scatter.9
  601.8 80.5 reduce-scatter.13
  684.7 91.5 reduce-scatter.11
  781.2 154.1 reduce-scatter.5
